TPU v7x, 8 devices: a whole 2x2x1 slice. The times are simulated.
8 devices in a mesh: data: 1 (over z), expert: 8 (over y, x, core).
Axes of the slice: x: 2, y: 2, z: 1, core: 2. Of those that a mesh axis runs over, the one named last changes fastest.
Arguments:
- x: bfloat16 [1024, 2048], P(('data', 'expert'))
- idx: int32 [1024, 8], P(('data', 'expert'))
- g: float32 [1024, 8], P(('data', 'expert'))
- hot_tok: int32 [512], P(('data', 'expert'))
- W1: bfloat16 [64, 2048, 1024], P('expert')
- W3: bfloat16 [64, 2048, 1024], P('expert')
- W2: bfloat16 [64, 1024, 2048], P('expert')
Outputs:
- output: bfloat16 [1024, 2048], P(('data', 'expert'))
All inputs are finite; a program needn't handle non-finite values.
Results may differ from a plain program's by a relative error of at most 0.001.
Values are sent between devices in bfloat16 or wider.
A program may use at most 1 GiB of HBM per device.

v0:
```python
import jax
import jax.numpy as jnp
from jax import lax
from jax.sharding import PartitionSpec as P


def _dest(idx, hot_tok, n, el, ch, cap):
    t, k = idx.shape
    s = ch + (el - 1) * cap
    flat = idx.reshape(-1)
    onehot = (flat[:, None] == jnp.arange(n * el, dtype=jnp.int32)[None, :]).astype(jnp.int32)
    rank = jnp.take_along_axis(jnp.cumsum(onehot, axis=0) - onehot, flat[:, None], axis=1).reshape(t, k)
    hot_rank = jnp.zeros((t,), jnp.int32).at[hot_tok].set(jnp.arange(ch, dtype=jnp.int32))
    loc = idx % el
    pos = (idx // el) * s + jnp.where(loc == 0, rank, ch + (loc - 1) * cap + rank)
    return jnp.where(idx == 0, hot_rank[:, None], pos)


def _send(x, dest, rows):
    t, d = x.shape
    k = dest.shape[1]
    src = jnp.full((rows,), t, jnp.int32).at[dest.reshape(-1)].set(jnp.repeat(jnp.arange(t, dtype=jnp.int32), k))
    return jnp.concatenate([x, jnp.zeros((1, d), x.dtype)])[src]


def _combine(back, dest, g):
    y = jnp.zeros((dest.shape[0], back.shape[1]), jnp.float32)
    for j in range(dest.shape[1]):
        y = y + g[:, j:j + 1] * back[dest[:, j]].astype(jnp.float32)
    return y.astype(jnp.bfloat16)


def _experts(xs, w1, w3, w2, form_in, form_out):
    a = jnp.einsum(form_in, xs, w1, preferred_element_type=jnp.float32)
    b = jnp.einsum(form_in, xs, w3, preferred_element_type=jnp.float32)
    u = (jax.nn.silu(a) * b).astype(jnp.bfloat16)
    return jnp.einsum(form_out, u, w2, preferred_element_type=jnp.float32).astype(jnp.bfloat16)


def solution(mesh):
    n = mesh.shape['expert']

    def local(x, idx, g, hot_tok, w1, w3, w2):
        t, d = x.shape
        k = idx.shape[1]
        el = w1.shape[0]
        e = el * n
        ch = hot_tok.shape[0]
        cap = 2 * ((t * k - ch + e - 2) // (e - 1))
        s = ch + (el - 1) * cap
        dest = _dest(idx, hot_tok, n, el, ch, cap)
        send = _send(x, dest, n * s).reshape(n, s, d)
        recv = lax.all_to_all(send, 'expert', 0, 0, tiled=True)
        out = _experts(recv[:, :ch], w1[0], w3[0], w2[0], 'rcd,df->rcf', 'rcf,fd->rcd')
        if el > 1:
            xc = recv[:, ch:].reshape(n, el - 1, cap, d)
            oc = _experts(xc, w1[1:], w3[1:], w2[1:], 'recd,edf->recf', 'recf,efd->recd')
            out = jnp.concatenate([out, oc.reshape(n, (el - 1) * cap, d)], axis=1)
        back = lax.all_to_all(out, 'expert', 0, 0, tiled=True)
        return _combine(back.reshape(n * s, d), dest, g)

    rows = P(('data', 'expert'))
    wspec = P('expert')
    return jax.shard_map(local, mesh=mesh, in_specs=(rows, rows, rows, rows, wspec, wspec, wspec), out_specs=rows, check_vma=False)
```

profile of v0, /device:TPU:0, one launch (start us, length us, event | category | flops | bytes accessed | tf_op | source)
XLA Modules:
  0.0 404.5 jit_solution(268331676851247324)
XLA Ops:
  0.0 0.7 broadcast_compare_fusion
  0.8 0.7 broadcast_add_fusion.1
  1.4 0.8 copy.26
  2.5 0.7 compare_select_fusion.11
  3.6 18.0 %reduce-window.6 = s32[64,8,128]{2,1,0:T(8,128)S(1)} reduce-window(s32[64,8,128]{2,1,0:T(8,128)S(1)} %fusion.45, s32[]{:T(128)} %constant.42.clone.1), window={size=1x1x128 pad=0_0x0_0x127_0}, to_apply=%region_1.2 | reduce-window | flops 8323072 | bytes 524292 | tf_op jit(solution)/shard_map/reduce-window
  21.7 0.1 copy.34
  22.0 0.1 broadcast_add_fusion
  22.2 8.6 %gather_fusion.9 = s32[1024]{0:T(1024)S(1)} fusion(s32[1024,64]{0,1:T(8,128)S(1)} %fusion.44, s32[1024]{0:T(1024)S(1)} %bitcast.93), kind=kCustom, calls=%fused_computation.9 | custom fusion | bytes 16384 | tf_op jit(solution)/shard_map/jit(take_along_axis)/gather | solution.py:12
  31.0 0.8 scatter_custom_fusion
  32.0 4.3 %scatter_custom_fusion.1 = s32[2304]{0:T(1024)S(1)} fusion(s32[1024]{0:T(1024)S(1)} %bitcast.100, s32[1024]{0:T(1024)S(1)} %reshape.239, s32[]{:T(128)} %constant.40.clone.1), kind=kCustom, calls=%fused_computation.86 | custom fusion | bytes 9220 | tf_op jit(solution)/shard_map/scatter | solution.py:22
  36.4 9.9 %gather_fusion = bf16[2304,2048]{1,0:T(8,128)(2,1)} fusion(bf16[129,2048]{1,0:T(8,128)(2,1)S(1)} %concatenate.6, s32[3072]{0:T(1024)S(1)} %pad_clamp_fusion), kind=kCustom, calls=%fused_computation | custom fusion | bytes 18883584 | tf_op jit(solution)/shard_map/gather | solution.py:23
  46.3 109.3 %all_to_all.10 = bf16[8,288,2048]{2,1,0:T(8,128)(2,1)S(1)} all-to-all(bf16[8,288,2048]{2,1,0:T(8,128)(2,1)} %bitcast.94), channel_id=1, replica_groups=mesh['data'=1,'expert'=8] {'expert'}, dimensions={0} | all-to-all | bytes 18874368 | tf_op jit(solution)/shard_map/all_to_all | solution.py:53
  155.6 4.7 %slice.129 = bf16[8,224,2048]{2,1,0:T(8,128)(2,1)} slice(bf16[8,288,2048]{2,1,0:T(8,128)(2,1)S(1)} %all_to_all.10), slice={[0:8], [64:288], [0:2048]} | slice | bytes 14680064 | tf_op jit(solution)/shard_map/slice | solution.py:56
  160.4 18.0 %fusion.2 = f32[7,8,32,1024]{3,2,1,0:T(8,128)} fusion(bf16[8,2048,1024]{2,1,0:T(8,128)(2,1)} %param.12, bf16[8,7,32,2048]{3,2,1,0:T(8,128)(2,1)} %bitcast.96), kind=kOutput, calls=%fused_computation.14 | convolution fusion | flops 7516192768 | bytes 44040192 | tf_op jit(solution)/shard_map/recd,edf->recf/dot_general | solution.py:35
  178.4 18.3 %fusion.9 = bf16[8,7,32,1024]{3,2,0,1:T(8,128)(2,1)} fusion(f32[7,8,32,1024]{3,2,1,0:T(8,128)} %fusion.2, bf16[8,2048,1024]{2,1,0:T(8,128)(2,1)} %param.11, bf16[8,7,32,2048]{3,2,1,0:T(8,128)(2,1)} %bitcast.97), kind=kOutput, calls=%fused_computation.23 | convolution fusion | flops 7527202816 | bytes 47710208 | tf_op jit(solution)/shard_map/recd,edf->recf/dot_general | solution.py:34
  196.7 14.0 %convert_bitcast_fusion = bf16[8,7,32,2048]{3,2,0,1:T(8,128)(2,1)S(1)} fusion(bf16[8,7,32,1024]{3,2,0,1:T(8,128)(2,1)} %fusion.9, bf16[8,1024,2048]{2,1,0:T(8,128)(2,1)} %param.13), kind=kOutput, calls=%fused_computation.29 | convolution fusion | flops 7519862784 | bytes 40370176 | tf_op jit(solution)/shard_map/recf,efd->recd/dot_general | solution.py:37
  210.7 4.4 %copy.41 = bf16[8,7,32,2048]{3,2,1,0:T(8,128)(2,1)} copy(bf16[8,7,32,2048]{3,2,0,1:T(8,128)(2,1)S(1)} %convert_bitcast_fusion) | data formatting | bytes 14680064 | tf_op jit(solution)/shard_map/convert_element_type | solution.py:37
  215.0 6.5 %fusion.23 = f32[8,64,1024]{2,1,0:T(8,128)} fusion(bf16[8,2048,1024]{2,1,0:T(8,128)(2,1)} %param.12, bf16[8,288,2048]{2,1,0:T(8,128)(2,1)} %copy-done), kind=kOutput, calls=%fused_computation.34 | convolution fusion | flops 2147483648 | bytes 8388608 | tf_op jit(solution)/shard_map/rcd,df->rcf/dot_general | solution.py:35
  221.5 9.3 %fusion.30 = bf16[8,64,2048]{2,1,0:T(8,128)(2,1)S(1)} fusion(bf16[8,1024,2048]{2,1,0:T(8,128)(2,1)} %param.13, f32[8,64,1024]{2,1,0:T(8,128)} %fusion.23, bf16[8,2048,1024]{2,1,0:T(8,128)(2,1)} %param.11, bf16[8,288,2048]{2,1,0:T(8,128)(2,1)} %copy-done), kind=kOutput, calls=%fused_computation.41 | convolution fusion | flops 4299161600 | bytes 14680064 | tf_op jit(solution)/shard_map/rcf,fd->rcd/dot_general | solution.py:37
  230.9 8.6 %pad_maximum_fusion = bf16[8,288,2048]{2,1,0:T(8,128)(2,1)} fusion(bf16[8,224,2048]{2,1,0:T(8,128)(2,1)} %bitcast.95, bf16[8,64,2048]{2,1,0:T(8,128)(2,1)S(1)} %fusion.30), kind=kLoop, calls=%fused_computation.21 | loop fusion | flops 18874368 | bytes 18874368 | tf_op jit(solution)/shard_map/concatenate | solution.py:58
  239.5 4.1 %all-to-all-start.1 = ((bf16[8,288,2048]{2,1,0:T(8,128)(2,1)}), bf16[8,288,2048]{2,1,0:T(8,128)(2,1)}, u32[]{:S(2)}, u32[]{:S(2)}) async-start(bf16[8,288,2048]{2,1,0:T(8,128)(2,1)} %pad_maximum_fusion), calls=%async_computation.1 | async-start | bytes 18874368 | tf_op jit(solution)/shard_map/all_to_all | solution.py:59
  243.6 0.4 fusion.49
  244.1 104.6 %all-to-all-done.1 = bf16[8,288,2048]{2,1,0:T(8,128)(2,1)} async-done(((bf16[8,288,2048]{2,1,0:T(8,128)(2,1)}), bf16[8,288,2048]{2,1,0:T(8,128)(2,1)}, u32[]{:S(2)}, u32[]{:S(2)}) %all-to-all-start.1) | async-done | bytes 9437216 | tf_op jit(solution)/shard_map/all_to_all | solution.py:59
  348.6 6.3 %gather_fusion.8 = bf16[128,2048]{1,0:T(8,128)(2,1)S(1)} fusion(bf16[2304,2048]{1,0:T(8,128)(2,1)} %bitcast.24, s32[1024]{0:T(1024)S(1)} %get-tuple-element.21), kind=kCustom, calls=%fused_computation.8 | custom fusion | bytes 1049088 | tf_op jit(solution)/shard_map/gather | solution.py:29
  355.0 6.3 %gather_fusion.7 = bf16[128,2048]{1,0:T(8,128)(2,1)S(1)} fusion(bf16[2304,2048]{1,0:T(8,128)(2,1)} %bitcast.24, s32[1024]{0:T(1024)S(1)} %get-tuple-element.22), kind=kCustom, calls=%fused_computation.7 | custom fusion | bytes 1049088 | tf_op jit(solution)/shard_map/gather | solution.py:29
  361.3 6.3 %gather_fusion.6 = bf16[128,2048]{1,0:T(8,128)(2,1)S(1)} fusion(bf16[2304,2048]{1,0:T(8,128)(2,1)} %bitcast.24, s32[1024]{0:T(1024)S(1)} %get-tuple-element.23), kind=kCustom, calls=%fused_computation.6 | custom fusion | bytes 1049088 | tf_op jit(solution)/shard_map/gather | solution.py:29
  367.7 6.3 %gather_fusion.5 = bf16[128,2048]{1,0:T(8,128)(2,1)S(1)} fusion(bf16[2304,2048]{1,0:T(8,128)(2,1)} %bitcast.24, s32[1024]{0:T(1024)S(1)} %get-tuple-element.24), kind=kCustom, calls=%fused_computation.5 | custom fusion | bytes 1049088 | tf_op jit(solution)/shard_map/gather | solution.py:29
  374.0 6.3 %gather_fusion.4 = bf16[128,2048]{1,0:T(8,128)(2,1)S(1)} fusion(bf16[2304,2048]{1,0:T(8,128)(2,1)} %bitcast.24, s32[1024]{0:T(1024)S(1)} %get-tuple-element.25), kind=kCustom, calls=%fused_computation.4 | custom fusion | bytes 1049088 | tf_op jit(solution)/shard_map/gather | solution.py:29
  380.3 6.6 %gather_fusion.3 = bf16[128,2048]{1,0:T(8,128)(2,1)S(1)} fusion(bf16[2304,2048]{1,0:T(8,128)(2,1)} %bitcast.24, s32[1024]{0:T(1024)S(1)} %get-tuple-element.26), kind=kCustom, calls=%fused_computation.3 | custom fusion | bytes 1049088 | tf_op jit(solution)/shard_map/gather | solution.py:29
  386.9 7.1 %gather_fusion.2 = bf16[128,2048]{1,0:T(8,128)(2,1)} fusion(bf16[2304,2048]{1,0:T(8,128)(2,1)} %bitcast.24, s32[1024]{0:T(1024)S(1)} %get-tuple-element.27), kind=kCustom, calls=%fused_computation.2 | custom fusion | bytes 1049088 | tf_op jit(solution)/shard_map/gather | solution.py:29
  394.1 7.1 %gather_fusion.1 = bf16[128,2048]{1,0:T(8,128)(2,1)} fusion(bf16[2304,2048]{1,0:T(8,128)(2,1)} %bitcast.24, s32[1024]{0:T(1024)S(1)} %get-tuple-element.28), kind=kCustom, calls=%fused_computation.1 | custom fusion | bytes 1049088 | tf_op jit(solution)/shard_map/gather | solution.py:29
  401.2 2.9 add_convert_fusion
  (36 shorter events, 1.4 us)
Async XLA Ops:
  0.0 36.3 %copy-start.1 = (bf16[128,2048]{1,0:T(8,128)(2,1)S(1)}, bf16[128,2048]{1,0:T(8,128)(2,1)}, u32[]{:S(2)}) copy-start(bf16[128,2048]{1,0:T(8,128)(2,1)} %param.7) | copy-start | bytes 1572868
  155.6 4.7 %copy-start = (bf16[8,288,2048]{2,1,0:T(8,128)(2,1)}, bf16[8,288,2048]{2,1,0:T(8,128)(2,1)S(1)}, u32[]{:S(2)}) copy-start(bf16[8,288,2048]{2,1,0:T(8,128)(2,1)S(1)} %all_to_all.10) | copy-start | bytes 28311556
  239.5 4.5 %copy-start.2 = (f32[128,8]{0,1:T(8,128)S(1)}, f32[128,8]{0,1:T(8,128)}, u32[]{:S(2)}) copy-start(f32[128,8]{0,1:T(8,128)} %param.9) | copy-start | bytes 12292
  239.5 109.1 %all-to-all-start.1 = ((bf16[8,288,2048]{2,1,0:T(8,128)(2,1)}), bf16[8,288,2048]{2,1,0:T(8,128)(2,1)}, u32[]{:S(2)}, u32[]{:S(2)}) async-start(bf16[8,288,2048]{2,1,0:T(8,128)(2,1)} %pad_maximum_fusion), calls=%async_computation.1 | async-start | bytes 18874368 | tf_op jit(solution)/shard_map/all_to_all | solution.py:59
where the time goes:
time: 412 us; the launch traced here: 404 us
  blocking collectives  109 us (26%)
  waiting for transfers between devices  105 us (25%)
  local copies, waits for them, and re-layouts  87.3 us (21%)
  matrix products  66.1 us (16%)
  other arithmetic  32.4 us (8%)
    all_to_all x1, blocking collectives, local(): recv = lax.all_to_all(send, 'expert', 0, 0, tiled=True)  109 us
    all_to_all x1, waiting for transfers between devices, local(): back = lax.all_to_all(out, 'expert', 0, 0, tiled=True)  105 us
    gather x8, local copies, waits for them, and re-layouts, _combine(): y = y + g[:, j:j + 1] * back[dest[:, j]].astype(jnp.float32)  52.5 us
    dot_general x2, matrix products, _experts(): b = jnp.einsum(form_in, xs, w3, preferred_element_type=jnp.float32)  24.5 us
    dot_general x2, matrix products, _experts(): jnp.einsum(form_out, u, w2, preferred_element_type=jnp.float32)  23.3 us
    dot_general x1, matrix products, _experts(): a = jnp.einsum(form_in, xs, w1, preferred_element_type=jnp.float32)  18.3 us
    another operation x3, other arithmetic  18.2 us
    gather x1, local copies, waits for them, and re-layouts, _send(): return jnp.concatenate([x, jnp.zeros((1, d), x.dtype)])[src]  9.93 us
  transfers between devices with their start and end apart: 1, of which 1 were waited for; matrix products, arithmetic and copies ran while one was open for 0% of the time, Pallas kernels for 0%

commit v1 on v0

v1 whole, which is shorter than its diff:
```python
import functools

import jax
import jax.numpy as jnp
from jax import lax
from jax.experimental import pallas as pl
from jax.experimental.pallas import tpu as pltpu
from jax.sharding import PartitionSpec as P

BF = jnp.bfloat16
F32 = jnp.float32
BF_MAX = 3.3895313892515355e38
T = 128
D = 2048
FF = 1024
EL = 8
N = 8
CAP = 32
RB = EL * CAP + CAP
KC = 4
KW = D // KC
NC = 8
NW = D // NC
NS = 6
FWD_AT = 5


def _dot(a, b):
    return jnp.dot(a, b, preferred_element_type=F32)


def _kernel(tab_ref, x_ref, w1_ref, w3_ref, w2_ref, y_ref,
            tabs, xall, onehot, gates, xs, acc, u, ring1, ring2, hbuf, ybuf, r1, r2, r3,
            tab_s, tab_r, ag_s, ag_r, w1_sem, w2_sem, d_s, d_r, s1_s, s1_r, s2_s, s2_r):
    me = lax.axis_index('expert')
    core, xb, yb = me % 2, (me // 2) % 2, me // 4

    def peer(mask):
        return {'expert': me + (mask & 1) * (1 - 2 * core) + ((mask >> 1) & 1) * (2 - 4 * xb) + (mask >> 2) * (4 - 8 * yb)}

    def remote(src, dst, ssem, rsem, mask):
        return pltpu.make_async_remote_copy(src_ref=src, dst_ref=dst, send_sem=ssem, recv_sem=rsem,
                                            device_id=peer(mask), device_id_type=pl.DeviceIdType.MESH)

    def up_copies(kc, e, slot):
        rows = pl.ds(kc * KW, KW)
        return (pltpu.make_async_copy(w1_ref.at[e, rows, :], ring1.at[slot, 0], w1_sem.at[slot, 0]),
                pltpu.make_async_copy(w3_ref.at[e, rows, :], ring1.at[slot, 1], w1_sem.at[slot, 1]))

    def down_copy(nc, e):
        return pltpu.make_async_copy(w2_ref.at[e, :, pl.ds(nc * NW, NW)], ring2.at[e], w2_sem.at[e])

    for i in range(NS):
        for c in up_copies(i // EL, i % EL, i):
            c.start()

    barrier = pltpu.get_barrier_semaphore()
    for mask in range(1, N):
        pl.semaphore_signal(barrier, inc=1, device_id=peer(mask), device_id_type=pl.DeviceIdType.MESH)
    pl.semaphore_wait(barrier, N - 1)

    def tab_copy(mask):
        return remote(tab_ref, tabs.at[mask], tab_s.at[mask], tab_r.at[mask], mask)

    def ag_copy(c, mask):
        return remote(x_ref.at[:, pl.ds(c * KW, KW)], xall.at[c, mask], ag_s.at[c, mask], ag_r.at[c, mask], mask)

    def fwd_copy(c, mask):
        return remote(xall.at[c, mask], xall.at[c, mask + 1], ag_s.at[c, mask + 1], ag_r.at[c, mask + 1], 1)

    for mask in range(1, N):
        tab_copy(mask).start()
    for c in range(KC):
        for mask in (6, 2, 4, 1):
            ag_copy(c, mask).start()
    tabs[0] = tab_ref[...]
    for c in range(KC):
        xall[c, 0] = x_ref[:, c * KW:(c + 1) * KW]
    for mask in range(1, N):
        tab_copy(mask).wait_recv()

    base = (me * EL).astype(F32)
    ids = lax.broadcasted_iota(jnp.int32, (EL, T), 0).astype(F32) + base
    sels, gs = [], []
    for r in range(N):
        sel = jnp.zeros((EL, T), F32)
        gate = jnp.zeros((EL, T), F32)
        tab = tabs[r]
        for j in range(8):
            hit = jnp.broadcast_to(tab[j:j + 1], (EL, T)) == ids
            sel = jnp.where(hit, 1.0, sel)
            gate = jnp.where(hit, jnp.broadcast_to(tab[8 + j:9 + j], (EL, T)), gate)
        sels.append(sel)
        gs.append(gate)
    sel_all = jnp.concatenate(sels, axis=0)
    upper = (lax.broadcasted_iota(jnp.int32, (T, T), 0) < lax.broadcasted_iota(jnp.int32, (T, T), 1))
    upper = jnp.where(upper, 1.0, 0.0).astype(BF)
    rank_all = jnp.where(sel_all > 0.5, _dot(sel_all.astype(BF), upper), -1.0)

    col = lax.broadcasted_iota(jnp.int32, (32, RB), 1)
    row = lax.broadcasted_iota(jnp.int32, (32, RB), 0)
    owner = jnp.where(col < EL * CAP, col // CAP, 0)
    pick = [jnp.where(row == q * EL + owner, 1.0, 0.0).astype(BF) for q in range(4)]
    colt = lax.broadcasted_iota(jnp.int32, (T, RB), 1)
    slot_of = jnp.where(colt < EL * CAP, colt % CAP, colt - EL * CAP + CAP).astype(F32)
    sub = lax.broadcasted_iota(jnp.int32, (CAP, T), 0).astype(F32)
    for r in range(N):
        rk = rank_all[r * EL:(r + 1) * EL]
        for b in range(EL + 1):
            want = sub if b < EL else sub + CAP
            src = b % EL
            hit = jnp.broadcast_to(rk[src:src + 1], (CAP, T)) == want
            onehot[r, b * CAP:(b + 1) * CAP, :] = jnp.where(hit, 1.0, 0.0).astype(BF)
        g = gs[r]
        g1 = jnp.minimum(g, BF_MAX).astype(BF).astype(F32)
        rem = g - g1
        g2 = rem.astype(BF).astype(F32)
        g3 = rem - g2
        v = jnp.concatenate([rk, g1, g2, g3], axis=0)
        vt = v.T.astype(BF)
        hit = _dot(vt, pick[0]) == slot_of
        for q in range(3):
            gates[r, q * T:(q + 1) * T, :] = jnp.where(hit, _dot(vt, pick[q + 1]), 0.0).astype(BF)

    def forward(c):
        for mask in (2, 4, 6):
            ag_copy(c, mask).wait_recv()
            fwd_copy(c, mask).start()

    forward(0)
    for kc in range(KC):
        ag_copy(kc, 1).wait_recv()
        for mask in (2, 4, 6):
            fwd_copy(kc, mask).wait_recv()

        def dispatch(r, _, kc=kc):
            rows = _dot(onehot[r], xall[kc, r]).astype(BF)
            at = pl.ds(pl.multiple_of(r * CAP, CAP), CAP)
            for b in range(EL + 1):
                xs[b, at, :] = rows[b * CAP:(b + 1) * CAP]
            return 0
        lax.fori_loop(0, N, dispatch, 0)

        def block(b, slot, kc=kc):
            xb_ = xs[b]
            for n in range(FF // 256):
                cols = slice(n * 256, (n + 1) * 256)
                a = _dot(xb_, ring1[slot, 0, :, cols])
                bb = _dot(xb_, ring1[slot, 1, :, cols])
                if kc > 0:
                    a = a + acc[0, b, :, cols]
                    bb = bb + acc[1, b, :, cols]
                if kc < KC - 1:
                    acc[0, b, :, cols] = a
                    acc[1, b, :, cols] = bb
                else:
                    u[b, :, cols] = (jax.nn.silu(a) * bb).astype(BF)

        def step(e, _, kc=kc):
            i = kc * EL + e
            slot = i % NS
            for c in up_copies(kc, e, slot):
                c.wait()
            block(e, slot)

            @pl.when(e == 0)
            def _():
                block(EL, slot)

            nxt = i + NS

            @pl.when(nxt < KC * EL)
            def _():
                for c in up_copies(nxt // EL, nxt % EL, slot):
                    c.start()

            if kc + 1 < KC:
                @pl.when(e == FWD_AT)
                def _():
                    forward(kc + 1)
            if kc == KC - 2:
                down_copy(0, e).start()
            return 0
        lax.fori_loop(0, EL, step, 0)

    def d_copy(nc):
        return remote(ybuf.at[nc % 2, 1], r1.at[nc], d_s.at[nc], d_r.at[nc], 1)

    def s1_copies(nc):
        return (remote(r1.at[nc, :, 1, pl.ds(0, 64), :], r2.at[nc, 0], s1_s.at[nc, 0], s1_r.at[nc, 0], 2),
                remote(r1.at[nc, 1, :, pl.ds(64, 64), :], r2.at[nc, 1], s1_s.at[nc, 1], s1_r.at[nc, 1], 4))

    def s2_copies(nc):
        return (remote(r2.at[nc, 0, 1], r3.at[nc, 0], s2_s.at[nc, 0], s2_r.at[nc, 0], 4),
                remote(r2.at[nc, 1, 1], r3.at[nc, 1], s2_s.at[nc, 1], s2_r.at[nc, 1], 2))

    def stage1(nc):
        d_copy(nc).wait_recv()
        for q in range(4):
            r1[nc, q // 2, q % 2] = r1[nc, q // 2, q % 2] + ybuf[nc % 2, 0, q // 2, q % 2]
        for c in s1_copies(nc):
            c.start()

    def stage2(nc):
        ca, cb = s1_copies(nc)
        sa, sb = s2_copies(nc)
        ca.wait_recv()
        r2[nc, 0, 1] = r2[nc, 0, 1] + r1[nc, 1, 0, 0:64]
        sa.start()
        cb.wait_recv()
        r2[nc, 1, 1] = r2[nc, 1, 1] + r1[nc, 0, 1, 64:128]
        sb.start()

    def final(nc):
        for h, c in enumerate(s2_copies(nc)):
            c.wait_recv()
            rows = slice(h * 64, h * 64 + 64)
            val = r1[nc, 0, 0, rows] + r2[nc, h, 0] + r3[nc, h]
            y_ref[rows, pl.ds(pl.multiple_of(nc * NW, NW), NW)] = val.astype(BF)

    def out_step(nc, _):
        def down(e, _):
            down_copy(nc, e).wait()

            def put(b):
                h = _dot(u[b], ring2[e]).astype(BF)
                at = pl.ds(pl.multiple_of(b * CAP, CAP), CAP)
                for r in range(N):
                    hbuf[r, at, :] = h[r * CAP:(r + 1) * CAP]
            put(e)

            @pl.when(e == 0)
            def _():
                put(EL)

            @pl.when(nc + 1 < NC)
            def _():
                down_copy(nc + 1, e).start()
            return 0
        lax.fori_loop(0, EL, down, 0)

        @pl.when(nc >= 2)
        def _():
            d_copy(nc - 2).wait_send()

        def combine(r, _):
            part = _dot(gates[r], hbuf[r])
            ybuf[nc % 2, r % 2, r // 4, (r // 2) % 2] = part[0:T] + part[T:2 * T] + part[2 * T:3 * T]
            return 0
        lax.fori_loop(0, N, combine, 0)
        d_copy(nc).start()

        @pl.when(nc >= 1)
        def _():
            stage1(nc - 1)

        @pl.when(nc >= 2)
        def _():
            stage2(nc - 2)

        @pl.when(nc >= 4)
        def _():
            final(nc - 4)
        return 0
    lax.fori_loop(0, NC, out_step, 0)
    stage1(NC - 1)
    stage2(NC - 2)
    final(NC - 4)
    final(NC - 3)
    stage2(NC - 1)
    final(NC - 2)
    final(NC - 1)

    for mask in range(1, N):
        tab_copy(mask).wait_send()
    for c in range(KC):
        for mask in (1, 2, 4, 6):
            ag_copy(c, mask).wait_send()
        for mask in (2, 4, 6):
            fwd_copy(c, mask).wait_send()
    for nc in range(NC):
        if nc >= NC - 2:
            d_copy(nc).wait_send()
        for c in s1_copies(nc) + s2_copies(nc):
            c.wait_send()


def _moe(tab, x, w1, w3, w2):
    dma = pltpu.SemaphoreType.DMA
    vm, hbm = pl.BlockSpec(memory_space=pltpu.VMEM), pl.BlockSpec(memory_space=pl.ANY)
    return pl.pallas_call(
        _kernel,
        out_shape=jax.ShapeDtypeStruct((T, D), BF),
        in_specs=[vm, vm, hbm, hbm, hbm],
        out_specs=vm,
        scratch_shapes=[
            pltpu.VMEM((N, 16, T), F32),
            pltpu.VMEM((KC, N, T, KW), BF),
            pltpu.VMEM((N, RB, T), BF),
            pltpu.VMEM((N, 3 * T, RB), BF),
            pltpu.VMEM((EL + 1, N * CAP, KW), BF),
            pltpu.VMEM((2, EL + 1, N * CAP, FF), F32),
            pltpu.VMEM((EL + 1, N * CAP, FF), BF),
            pltpu.VMEM((NS, 2, KW, FF), BF),
            pltpu.VMEM((EL, FF, NW), BF),
            pltpu.VMEM((N, RB, NW), BF),
            pltpu.VMEM((2, 2, 2, 2, T, NW), F32),
            pltpu.VMEM((NC, 2, 2, T, NW), F32),
            pltpu.VMEM((NC, 2, 2, 64, NW), F32),
            pltpu.VMEM((NC, 2, 64, NW), F32),
            dma((N,)), dma((N,)),
            dma((KC, N)), dma((KC, N)),
            dma((NS, 2)), dma((EL,)),
            dma((NC,)), dma((NC,)),
            dma((NC, 2)), dma((NC, 2)),
            dma((NC, 2)), dma((NC, 2)),
        ],
        compiler_params=pltpu.CompilerParams(collective_id=0, has_side_effects=True, vmem_limit_bytes=67043328),
        name='moe',
    )(tab, x, w1, w3, w2)


def solution(mesh):
    def local(x, idx, g, hot_tok, w1, w3, w2):
        tab = jnp.concatenate([idx.T.astype(F32), g.T], axis=0)
        return _moe(tab, x, w1, w3, w2)

    rows = P(('data', 'expert'))
    wspec = P('expert')
    return jax.shard_map(local, mesh=mesh, in_specs=(rows, rows, rows, rows, wspec, wspec, wspec), out_specs=rows, check_vma=False)
```

time: 412 us -> 111 us (0.27); the launches traced: 404 us -> 110 us
  blocking collectives: 109 us -> 0 us
  Pallas kernels: 0 us -> 107 us
  waiting for transfers between devices: 105 us -> 0 us
  local copies, waits for them, and re-layouts: 87.3 us -> 1.88 us
  matrix products: 66.1 us -> 0 us
  other arithmetic: 32.4 us -> 1.97 us
    all_to_all x1 -> x0, blocking collectives: 109 us -> none  [local(): recv = lax.all_to_all(send, 'expert', 0, 0, tiled=True)]
    pallas_call x0 -> x1, Pallas kernels: none -> 107 us  [_moe(): pl.pallas_call(_kernel, out_shape=jax.ShapeDtypeStruct((T, D), BF), in_sp...]
    all_to_all x1 -> x0, waiting for transfers between devices: 105 us -> none  [local(): back = lax.all_to_all(out, 'expert', 0, 0, tiled=True)]
    gather x11 -> x0, local copies, waits for them, and re-layouts: 71.2 us -> none  [the longest x8 52.5 us: _combine(): y = y + g[:, j:j + 1] * back[dest[:, j]].astype(jnp.float32)]
    dot_general x5 -> x0, matrix products: 66.1 us -> none  [the longest x2 24.5 us: _experts(): b = jnp.einsum(form_in, xs, w3, preferred_element_type=jnp.float32)]
    another operation x3 -> x0, other arithmetic: 18.2 us -> none
    concatenate x1, other arithmetic: 8.64 us -> 1.29 us  [local(): tab = jnp.concatenate([idx.T.astype(F32), g.T], axis=0)]
    scatter x2 -> x0, local copies, waits for them, and re-layouts: 5.1 us -> none  [the longest x1 4.33 us: _send(): jnp.full((rows,), t, jnp.int32).at[dest.reshape(-1)]]
  transfers between devices with their start and end apart: 1 -> 0, of which waited for: 1 -> 0; matrix products, arithmetic and copies ran while one was open for 0% -> 0% of each run, Pallas kernels for 0% -> 0%
where the time goes in v1:
time: 111 us; the launch traced here: 110 us
  Pallas kernels  107 us (96%)
  other arithmetic  1.97 us (2%)
  local copies, waits for them, and re-layouts  1.88 us (2%)
    pallas_call x1, Pallas kernels, _moe(): pl.pallas_call(_kernel, out_shape=jax.ShapeDtypeStruct((T, D), BF), in_sp...  107 us

profile of v1, /device:TPU:0, one launch (start us, length us, event | category | flops | bytes accessed | tf_op | source)
XLA Modules:
  0.0 110.4 jit_solution(17700051794615850644)
XLA Ops:
  0.0 0.7 convert_bitcast_fusion
  0.7 1.3 %pad_maximum_fusion.tab_ref = f32[16,128]{1,0:T(8,128)} fusion(f32[8,128]{1,0:T(8,128)} %bitcast.3, f32[8,128]{1,0:T(8,128)S(1)} %convert_bitcast_fusion), kind=kLoop, calls=%fused_computation | loop fusion | flops 2048 | bytes 16384 | tf_op jit(solution)/shard_map/concatenate | solution.py:325
  2.0 106.6 %moe.1 = bf16[128,2048]{1,0:T(8,128)(2,1)} custom-call(f32[16,128]{1,0:T(8,128)} %pad_maximum_fusion.tab_ref, bf16[128,2048]{1,0:T(8,128)(2,1)} %x_ref.1, bf16[8,2048,1024]{2,1,0:T(8,128)(2,1)} %w1_ref.1, bf16[8,2048,1024]{2,1,0:T(8,128)(2,1)} %w3_ref.1, bf16[8,1024,2048]{2,1,0:T(8,128)(2,1)} %w2_ref.1), custom_call_target="tpu_custom_call" | custom-call | tf_op jit(solution)/shard_map/moe/pallas_call | solution.py:291
  108.5 1.9 %copy.8 = bf16[128,2048]{1,0:T(8,128)(2,1)} copy(bf16[128,2048]{1,0:T(8,128)(2,1)} %moe.1) | data formatting | bytes 1048576

commit v2 on v1

--- a/solution.py
+++ b/solution.py
@@ -21,8 +21,11 @@
 KW = D // KC
 NC = 8
 NW = D // NC
-NS = 6
-FWD_AT = 5
+EP = 2
+NP = EL // EP
+NS = 3
+FWD_AT = 2
+CHIP = (0, 3, 1, 2)
 
 
 def _dot(a, b):
@@ -30,7 +33,7 @@
 
 
 def _kernel(tab_ref, x_ref, w1_ref, w3_ref, w2_ref, y_ref,
-            tabs, xall, onehot, gates, xs, acc, u, ring1, ring2, hbuf, ybuf, r1, r2, r3,
+            tabs, xall, onehot, gates, xs, acc, u, ring1, ring2, hbuf, r1, r2, r3,
             tab_s, tab_r, ag_s, ag_r, w1_sem, w2_sem, d_s, d_r, s1_s, s1_r, s2_s, s2_r):
     me = lax.axis_index('expert')
     core, xb, yb = me % 2, (me // 2) % 2, me // 4
@@ -42,16 +45,17 @@
         return pltpu.make_async_remote_copy(src_ref=src, dst_ref=dst, send_sem=ssem, recv_sem=rsem,
                                             device_id=peer(mask), device_id_type=pl.DeviceIdType.MESH)
 
-    def up_copies(kc, e, slot):
+    def up_copies(kc, p, slot):
         rows = pl.ds(kc * KW, KW)
-        return (pltpu.make_async_copy(w1_ref.at[e, rows, :], ring1.at[slot, 0], w1_sem.at[slot, 0]),
-                pltpu.make_async_copy(w3_ref.at[e, rows, :], ring1.at[slot, 1], w1_sem.at[slot, 1]))
-
-    def down_copy(nc, e):
-        return pltpu.make_async_copy(w2_ref.at[e, :, pl.ds(nc * NW, NW)], ring2.at[e], w2_sem.at[e])
+        es = pl.ds(p * EP, EP)
+        return (pltpu.make_async_copy(w1_ref.at[es, rows, :], ring1.at[slot, 0], w1_sem.at[slot, 0]),
+                pltpu.make_async_copy(w3_ref.at[es, rows, :], ring1.at[slot, 1], w1_sem.at[slot, 1]))
+
+    def down_copy(nc):
+        return pltpu.make_async_copy(w2_ref.at[:, :, pl.ds(nc * NW, NW)], ring2.at[nc % 2], w2_sem.at[nc % 2])
 
     for i in range(NS):
-        for c in up_copies(i // EL, i % EL, i):
+        for c in up_copies(i // NP, i % NP, i):
             c.start()
 
     barrier = pltpu.get_barrier_semaphore()
@@ -133,20 +137,17 @@
         for mask in (2, 4, 6):
             fwd_copy(kc, mask).wait_recv()
 
-        def dispatch(r, _, kc=kc):
+        for r in range(N):
             rows = _dot(onehot[r], xall[kc, r]).astype(BF)
-            at = pl.ds(pl.multiple_of(r * CAP, CAP), CAP)
             for b in range(EL + 1):
-                xs[b, at, :] = rows[b * CAP:(b + 1) * CAP]
-            return 0
-        lax.fori_loop(0, N, dispatch, 0)
-
-        def block(b, slot, kc=kc):
+                xs[b, r * CAP:(r + 1) * CAP, :] = rows[b * CAP:(b + 1) * CAP]
+
+        def block(b, slot, q, kc=kc):
             xb_ = xs[b]
             for n in range(FF // 256):
                 cols = slice(n * 256, (n + 1) * 256)
-                a = _dot(xb_, ring1[slot, 0, :, cols])
-                bb = _dot(xb_, ring1[slot, 1, :, cols])
+                a = _dot(xb_, ring1[slot, 0, q, :, cols])
+                bb = _dot(xb_, ring1[slot, 1, q, :, cols])
                 if kc > 0:
                     a = a + acc[0, b, :, cols]
                     bb = bb + acc[1, b, :, cols]
@@ -156,48 +157,51 @@
                 else:
                     u[b, :, cols] = (jax.nn.silu(a) * bb).astype(BF)
 
-        def step(e, _, kc=kc):
-            i = kc * EL + e
+        def step(p, _, kc=kc):
+            i = kc * NP + p
             slot = i % NS
-            for c in up_copies(kc, e, slot):
+            for c in up_copies(kc, p, slot):
                 c.wait()
-            block(e, slot)
-
-            @pl.when(e == 0)
+            for q in range(EP):
+                block(p * EP + q, slot, q)
+
+            @pl.when((p == 0) & (me == 0))
             def _():
-                block(EL, slot)
+                block(EL, slot, 0)
 
             nxt = i + NS
 
-            @pl.when(nxt < KC * EL)
+            @pl.when(nxt < KC * NP)
             def _():
-                for c in up_copies(nxt // EL, nxt % EL, slot):
+                for c in up_copies(nxt // NP, nxt % NP, slot):
                     c.start()
 
             if kc + 1 < KC:
-                @pl.when(e == FWD_AT)
+                @pl.when(p == FWD_AT)
                 def _():
                     forward(kc + 1)
-            if kc == KC - 2:
-                down_copy(0, e).start()
+            if kc == KC - 1:
+                @pl.when(p < 2)
+                def _():
+                    down_copy(p).start()
             return 0
-        lax.fori_loop(0, EL, step, 0)
+        lax.fori_loop(0, NP, step, 0)
 
     def d_copy(nc):
-        return remote(ybuf.at[nc % 2, 1], r1.at[nc], d_s.at[nc], d_r.at[nc], 1)
+        return remote(acc.at[nc % 2, pl.ds(4, 4), pl.ds(0, T), pl.ds(0, NW)], r1.at[nc], d_s.at[nc], d_r.at[nc], 1)
 
     def s1_copies(nc):
-        return (remote(r1.at[nc, :, 1, pl.ds(0, 64), :], r2.at[nc, 0], s1_s.at[nc, 0], s1_r.at[nc, 0], 2),
-                remote(r1.at[nc, 1, :, pl.ds(64, 64), :], r2.at[nc, 1], s1_s.at[nc, 1], s1_r.at[nc, 1], 4))
+        return (remote(r1.at[nc, pl.ds(2, 2), pl.ds(0, 64), :], r2.at[nc, 0], s1_s.at[nc, 0], s1_r.at[nc, 0], 2),
+                remote(r1.at[nc, pl.ds(1, 2), pl.ds(64, 64), :], r2.at[nc, 1], s1_s.at[nc, 1], s1_r.at[nc, 1], 4))
 
     def s2_copies(nc):
-        return (remote(r2.at[nc, 0, 1], r3.at[nc, 0], s2_s.at[nc, 0], s2_r.at[nc, 0], 4),
+        return (remote(r2.at[nc, 0, 0], r3.at[nc, 0], s2_s.at[nc, 0], s2_r.at[nc, 0], 4),
                 remote(r2.at[nc, 1, 1], r3.at[nc, 1], s2_s.at[nc, 1], s2_r.at[nc, 1], 2))
 
     def stage1(nc):
         d_copy(nc).wait_recv()
         for q in range(4):
-            r1[nc, q // 2, q % 2] = r1[nc, q // 2, q % 2] + ybuf[nc % 2, 0, q // 2, q % 2]
+            r1[nc, q] = r1[nc, q] + acc[nc % 2, q, 0:T, 0:NW]
         for c in s1_copies(nc):
             c.start()
 
@@ -205,71 +209,77 @@
         ca, cb = s1_copies(nc)
         sa, sb = s2_copies(nc)
         ca.wait_recv()
-        r2[nc, 0, 1] = r2[nc, 0, 1] + r1[nc, 1, 0, 0:64]
+        r2[nc, 0, 0] = r2[nc, 0, 0] + r1[nc, 1, 0:64]
         sa.start()
         cb.wait_recv()
-        r2[nc, 1, 1] = r2[nc, 1, 1] + r1[nc, 0, 1, 64:128]
+        r2[nc, 1, 1] = r2[nc, 1, 1] + r1[nc, 3, 64:128]
         sb.start()
 
     def final(nc):
         for h, c in enumerate(s2_copies(nc)):
             c.wait_recv()
             rows = slice(h * 64, h * 64 + 64)
-            val = r1[nc, 0, 0, rows] + r2[nc, h, 0] + r3[nc, h]
+            val = r1[nc, 0, rows] + r2[nc, h, 1 - h] + r3[nc, h]
             y_ref[rows, pl.ds(pl.multiple_of(nc * NW, NW), NW)] = val.astype(BF)
 
     def out_step(nc, _):
-        def down(e, _):
-            down_copy(nc, e).wait()
-
-            def put(b):
-                h = _dot(u[b], ring2[e]).astype(BF)
-                at = pl.ds(pl.multiple_of(b * CAP, CAP), CAP)
-                for r in range(N):
-                    hbuf[r, at, :] = h[r * CAP:(r + 1) * CAP]
-            put(e)
-
-            @pl.when(e == 0)
-            def _():
-                put(EL)
-
-            @pl.when(nc + 1 < NC)
-            def _():
-                down_copy(nc + 1, e).start()
-            return 0
-        lax.fori_loop(0, EL, down, 0)
+        down_copy(nc).wait()
+
+        def put(b, e):
+            h = _dot(u[b], ring2[nc % 2, e]).astype(BF)
+            for r in range(N):
+                hbuf[r, b * CAP:(b + 1) * CAP, :] = h[r * CAP:(r + 1) * CAP]
+        for e in range(EL):
+            put(e, e)
+
+        @pl.when(me == 0)
+        def _():
+            put(EL, 0)
+
+        @pl.when(nc + 2 < NC)
+        def _():
+            down_copy(nc + 2).start()
+
+        @pl.when(nc >= 1)
+        def _():
+            stage1(nc - 1)
 
         @pl.when(nc >= 2)
         def _():
             d_copy(nc - 2).wait_send()
 
-        def combine(r, _):
-            part = _dot(gates[r], hbuf[r])
-            ybuf[nc % 2, r % 2, r // 4, (r // 2) % 2] = part[0:T] + part[T:2 * T] + part[2 * T:3 * T]
-            return 0
-        lax.fori_loop(0, N, combine, 0)
+        def combine(rows):
+            for r in range(N):
+                part = _dot(gates[r, :, 0:rows], hbuf[r, 0:rows, :])
+                acc[nc % 2, 4 * (r % 2) + CHIP[r // 2], 0:T, 0:NW] = part[0:T] + part[T:2 * T] + part[2 * T:3 * T]
+
+        @pl.when(me == 0)
+        def _():
+            combine(RB)
+
+        @pl.when(me != 0)
+        def _():
+            combine(EL * CAP)
+
         d_copy(nc).start()
 
-        @pl.when(nc >= 1)
-        def _():
-            stage1(nc - 1)
-
-        @pl.when(nc >= 2)
-        def _():
-            stage2(nc - 2)
-
-        @pl.when(nc >= 4)
-        def _():
-            final(nc - 4)
+        @pl.when(nc >= 3)
+        def _():
+            stage2(nc - 3)
+
+        @pl.when(nc >= 5)
+        def _():
+            final(nc - 5)
         return 0
     lax.fori_loop(0, NC, out_step, 0)
     stage1(NC - 1)
+    stage2(NC - 3)
+    final(NC - 5)
     stage2(NC - 2)
     final(NC - 4)
-    final(NC - 3)
     stage2(NC - 1)
-    final(NC - 2)
-    final(NC - 1)
+    for nc in range(NC - 3, NC):
+        final(nc)
 
     for mask in range(1, N):
         tab_copy(mask).wait_send()
@@ -301,16 +311,15 @@
             pltpu.VMEM((EL + 1, N * CAP, KW), BF),
             pltpu.VMEM((2, EL + 1, N * CAP, FF), F32),
             pltpu.VMEM((EL + 1, N * CAP, FF), BF),
-            pltpu.VMEM((NS, 2, KW, FF), BF),
-            pltpu.VMEM((EL, FF, NW), BF),
+            pltpu.VMEM((NS, 2, EP, KW, FF), BF),
+            pltpu.VMEM((2, EL, FF, NW), BF),
             pltpu.VMEM((N, RB, NW), BF),
-            pltpu.VMEM((2, 2, 2, 2, T, NW), F32),
-            pltpu.VMEM((NC, 2, 2, T, NW), F32),
+            pltpu.VMEM((NC, 4, T, NW), F32),
             pltpu.VMEM((NC, 2, 2, 64, NW), F32),
             pltpu.VMEM((NC, 2, 64, NW), F32),
             dma((N,)), dma((N,)),
             dma((KC, N)), dma((KC, N)),
-            dma((NS, 2)), dma((EL,)),
+            dma((NS, 2)), dma((2,)),
             dma((NC,)), dma((NC,)),
             dma((NC, 2)), dma((NC, 2)),
             dma((NC, 2)), dma((NC, 2)),

time: 111 us -> 89.6 us (0.81)
  Pallas kernels: 107 us -> 85.5 us
    pallas_call x1, Pallas kernels: 107 us -> 85.5 us  [_moe(): pl.pallas_call(_kernel, out_shape=jax.ShapeDtypeStruct((T, D), BF), in_sp...]
where the time goes in v2:
time: 89.6 us; the launch traced here: 89.4 us
  Pallas kernels  85.5 us (95%)
  other arithmetic  1.97 us (2%)
  local copies, waits for them, and re-layouts  1.88 us (2%)
    pallas_call x1, Pallas kernels, _moe(): pl.pallas_call(_kernel, out_shape=jax.ShapeDtypeStruct((T, D), BF), in_sp...  85.5 us
    unnamed x1, local copies, waits for them, and re-layouts  1.88 us

profile of v2, /device:TPU:0, one launch (start us, length us, event | category | flops | bytes accessed | tf_op | source)
XLA Modules:
  0.0 89.4 jit_solution(4992335821455487813)
XLA Ops:
  0.0 0.7 convert_bitcast_fusion
  0.7 1.3 %pad_maximum_fusion.tab_ref = f32[16,128]{1,0:T(8,128)} fusion(f32[8,128]{1,0:T(8,128)} %bitcast.3, f32[8,128]{1,0:T(8,128)S(1)} %convert_bitcast_fusion), kind=kLoop, calls=%fused_computation | loop fusion | flops 2048 | bytes 16384 | tf_op jit(solution)/shard_map/concatenate | solution.py:334
  2.0 85.5 %moe.1 = bf16[128,2048]{1,0:T(8,128)(2,1)} custom-call(f32[16,128]{1,0:T(8,128)} %pad_maximum_fusion.tab_ref, bf16[128,2048]{1,0:T(8,128)(2,1)} %x_ref.1, bf16[8,2048,1024]{2,1,0:T(8,128)(2,1)} %w1_ref.1, bf16[8,2048,1024]{2,1,0:T(8,128)(2,1)} %w3_ref.1, bf16[8,1024,2048]{2,1,0:T(8,128)(2,1)} %w2_ref.1), custom_call_target="tpu_custom_call" | custom-call | tf_op jit(solution)/shard_map/moe/pallas_call | solution.py:301
  87.5 1.9 %copy.8 = bf16[128,2048]{1,0:T(8,128)(2,1)} copy(bf16[128,2048]{1,0:T(8,128)(2,1)} %moe.1) | data formatting | bytes 1048576

commit v3 on v2

--- a/solution.py
+++ b/solution.py
@@ -17,8 +17,9 @@
 N = 8
 CAP = 32
 RB = EL * CAP + CAP
-KC = 4
-KW = D // KC
+CHUNKS = ((0, 256), (256, 256), (512, 512), (1024, 512), (1536, 512))
+KC = len(CHUNKS)
+KW = 512
 NC = 8
 NW = D // NC
 EP = 2
@@ -32,9 +33,9 @@
     return jnp.dot(a, b, preferred_element_type=F32)
 
 
-def _kernel(tab_ref, x_ref, w1_ref, w3_ref, w2_ref, y_ref,
-            tabs, xall, onehot, gates, xs, acc, u, ring1, ring2, hbuf, r1, r2, r3,
-            tab_s, tab_r, ag_s, ag_r, w1_sem, w2_sem, d_s, d_r, s1_s, s1_r, s2_s, s2_r):
+def _kernel(idx_ref, g_ref, x_ref, w1_ref, w3_ref, w2_ref, y_ref,
+            idxs, gs, xsmall, xbig, onehot, gates, xs, acc, u, ring1, ring2, hbuf, r1, r2, r3,
+            tab_s, tab_r, gt_s, gt_r, ag_s, ag_r, w1_sem, w2_sem, d_s, d_r, s1_s, s1_r, s2_s, s2_r):
     me = lax.axis_index('expert')
     core, xb, yb = me % 2, (me // 2) % 2, me // 4
 
@@ -46,16 +47,17 @@
                                             device_id=peer(mask), device_id_type=pl.DeviceIdType.MESH)
 
     def up_copies(kc, p, slot):
-        rows = pl.ds(kc * KW, KW)
+        rows = pl.ds(*CHUNKS[kc])
+        to = pl.ds(0, CHUNKS[kc][1])
         es = pl.ds(p * EP, EP)
-        return (pltpu.make_async_copy(w1_ref.at[es, rows, :], ring1.at[slot, 0], w1_sem.at[slot, 0]),
-                pltpu.make_async_copy(w3_ref.at[es, rows, :], ring1.at[slot, 1], w1_sem.at[slot, 1]))
+        return (pltpu.make_async_copy(w1_ref.at[es, rows, :], ring1.at[slot, 0, :, to, :], w1_sem.at[slot, 0]),
+                pltpu.make_async_copy(w3_ref.at[es, rows, :], ring1.at[slot, 1, :, to, :], w1_sem.at[slot, 1]))
 
     def down_copy(nc):
         return pltpu.make_async_copy(w2_ref.at[:, :, pl.ds(nc * NW, NW)], ring2.at[nc % 2], w2_sem.at[nc % 2])
 
     for i in range(NS):
-        for c in up_copies(i // NP, i % NP, i):
+        for c in up_copies(0, i, i):
             c.start()
 
     barrier = pltpu.get_barrier_semaphore()
@@ -63,39 +65,56 @@
         pl.semaphore_signal(barrier, inc=1, device_id=peer(mask), device_id_type=pl.DeviceIdType.MESH)
     pl.semaphore_wait(barrier, N - 1)
 
-    def tab_copy(mask):
-        return remote(tab_ref, tabs.at[mask], tab_s.at[mask], tab_r.at[mask], mask)
+    def table_copies(mask):
+        return (remote(idx_ref, idxs.at[mask], tab_s.at[mask], tab_r.at[mask], mask),
+                remote(g_ref, gs.at[mask], gt_s.at[mask], gt_r.at[mask], mask))
+
+    def table_fwd(mask):
+        return (remote(idxs.at[mask], idxs.at[mask + 1], tab_s.at[mask + 1], tab_r.at[mask + 1], 1),
+                remote(gs.at[mask], gs.at[mask + 1], gt_s.at[mask + 1], gt_r.at[mask + 1], 1))
+
+    def part(c, mask):
+        return xsmall.at[c, mask] if c < 2 else xbig.at[c - 2, mask]
 
     def ag_copy(c, mask):
-        return remote(x_ref.at[:, pl.ds(c * KW, KW)], xall.at[c, mask], ag_s.at[c, mask], ag_r.at[c, mask], mask)
+        return remote(x_ref.at[:, pl.ds(*CHUNKS[c])], part(c, mask), ag_s.at[c, mask], ag_r.at[c, mask], mask)
 
     def fwd_copy(c, mask):
-        return remote(xall.at[c, mask], xall.at[c, mask + 1], ag_s.at[c, mask + 1], ag_r.at[c, mask + 1], 1)
-
-    for mask in range(1, N):
-        tab_copy(mask).start()
+        return remote(part(c, mask), part(c, mask + 1), ag_s.at[c, mask + 1], ag_r.at[c, mask + 1], 1)
+
+    for mask in (6, 2, 4, 1):
+        for c in table_copies(mask):
+            c.start()
     for c in range(KC):
         for mask in (6, 2, 4, 1):
             ag_copy(c, mask).start()
-    tabs[0] = tab_ref[...]
-    for c in range(KC):
-        xall[c, 0] = x_ref[:, c * KW:(c + 1) * KW]
-    for mask in range(1, N):
-        tab_copy(mask).wait_recv()
-
-    base = (me * EL).astype(F32)
-    ids = lax.broadcasted_iota(jnp.int32, (EL, T), 0).astype(F32) + base
-    sels, gs = [], []
+    idxs[0] = idx_ref[...]
+    gs[0] = g_ref[...]
+    for c, (first, width) in enumerate(CHUNKS):
+        part(c, 0)[...] = x_ref[:, first:first + width]
+    for mask in (2, 4, 6):
+        for c in table_copies(mask):
+            c.wait_recv()
+        for c in table_fwd(mask):
+            c.start()
+    for c in table_copies(1):
+        c.wait_recv()
+    for mask in (2, 4, 6):
+        for c in table_fwd(mask):
+            c.wait_recv()
+
+    ids = lax.broadcasted_iota(jnp.int32, (EL, T), 0) + me * EL
+    sels, weights = [], []
     for r in range(N):
         sel = jnp.zeros((EL, T), F32)
         gate = jnp.zeros((EL, T), F32)
-        tab = tabs[r]
+        tab, gtab = idxs[r], gs[r]
         for j in range(8):
             hit = jnp.broadcast_to(tab[j:j + 1], (EL, T)) == ids
             sel = jnp.where(hit, 1.0, sel)
-            gate = jnp.where(hit, jnp.broadcast_to(tab[8 + j:9 + j], (EL, T)), gate)
+            gate = jnp.where(hit, jnp.broadcast_to(gtab[j:j + 1], (EL, T)), gate)
         sels.append(sel)
-        gs.append(gate)
+        weights.append(gate)
     sel_all = jnp.concatenate(sels, axis=0)
     upper = (lax.broadcasted_iota(jnp.int32, (T, T), 0) < lax.broadcasted_iota(jnp.int32, (T, T), 1))
     upper = jnp.where(upper, 1.0, 0.0).astype(BF)
@@ -115,7 +134,7 @@
             src = b % EL
             hit = jnp.broadcast_to(rk[src:src + 1], (CAP, T)) == want
             onehot[r, b * CAP:(b + 1) * CAP, :] = jnp.where(hit, 1.0, 0.0).astype(BF)
-        g = gs[r]
+        g = weights[r]
         g1 = jnp.minimum(g, BF_MAX).astype(BF).astype(F32)
         rem = g - g1
         g2 = rem.astype(BF).astype(F32)
@@ -137,17 +156,18 @@
         for mask in (2, 4, 6):
             fwd_copy(kc, mask).wait_recv()
 
+        width = CHUNKS[kc][1]
         for r in range(N):
-            rows = _dot(onehot[r], xall[kc, r]).astype(BF)
+            rows = _dot(onehot[r], part(kc, r)[...]).astype(BF)
             for b in range(EL + 1):
-                xs[b, r * CAP:(r + 1) * CAP, :] = rows[b * CAP:(b + 1) * CAP]
-
-        def block(b, slot, q, kc=kc):
-            xb_ = xs[b]
+                xs[b, r * CAP:(r + 1) * CAP, 0:width] = rows[b * CAP:(b + 1) * CAP]
+
+        def block(b, slot, q, kc=kc, width=width):
+            rows = xs[b, :, 0:width]
             for n in range(FF // 256):
                 cols = slice(n * 256, (n + 1) * 256)
-                a = _dot(xb_, ring1[slot, 0, q, :, cols])
-                bb = _dot(xb_, ring1[slot, 1, q, :, cols])
+                a = _dot(rows, ring1[slot, 0, q, 0:width, cols])
+                bb = _dot(rows, ring1[slot, 1, q, 0:width, cols])
                 if kc > 0:
                     a = a + acc[0, b, :, cols]
                     bb = bb + acc[1, b, :, cols]
@@ -169,12 +189,16 @@
             def _():
                 block(EL, slot, 0)
 
-            nxt = i + NS
-
-            @pl.when(nxt < KC * NP)
+            @pl.when(p < NP - NS)
             def _():
-                for c in up_copies(nxt // NP, nxt % NP, slot):
+                for c in up_copies(kc, p + NS, slot):
                     c.start()
+
+            if kc + 1 < KC:
+                @pl.when(p >= NP - NS)
+                def _():
+                    for c in up_copies(kc + 1, p + NS - NP, slot):
+                        c.start()
 
             if kc + 1 < KC:
                 @pl.when(p == FWD_AT)
@@ -249,9 +273,11 @@
             d_copy(nc - 2).wait_send()
 
         def combine(rows):
-            for r in range(N):
-                part = _dot(gates[r, :, 0:rows], hbuf[r, 0:rows, :])
-                acc[nc % 2, 4 * (r % 2) + CHIP[r // 2], 0:T, 0:NW] = part[0:T] + part[T:2 * T] + part[2 * T:3 * T]
+            for r in (1, 3, 5, 7, 0, 2, 4, 6):
+                z = _dot(gates[r, :, 0:rows], hbuf[r, 0:rows, :])
+                acc[nc % 2, 4 * (r % 2) + CHIP[r // 2], 0:T, 0:NW] = z[0:T] + z[T:2 * T] + z[2 * T:3 * T]
+                if r == 7:
+                    d_copy(nc).start()
 
         @pl.when(me == 0)
         def _():
@@ -260,8 +286,6 @@
         @pl.when(me != 0)
         def _():
             combine(EL * CAP)
-
-        d_copy(nc).start()
 
         @pl.when(nc >= 3)
         def _():
@@ -281,8 +305,12 @@
     for nc in range(NC - 3, NC):
         final(nc)
 
-    for mask in range(1, N):
-        tab_copy(mask).wait_send()
+    for mask in (1, 2, 4, 6):
+        for c in table_copies(mask):
+            c.wait_send()
+    for mask in (2, 4, 6):
+        for c in table_fwd(mask):
+            c.wait_send()
     for c in range(KC):
         for mask in (1, 2, 4, 6):
             ag_copy(c, mask).wait_send()
@@ -295,17 +323,19 @@
             c.wait_send()
 
 
-def _moe(tab, x, w1, w3, w2):
+def _moe(idx, g, x, w1, w3, w2):
     dma = pltpu.SemaphoreType.DMA
     vm, hbm = pl.BlockSpec(memory_space=pltpu.VMEM), pl.BlockSpec(memory_space=pl.ANY)
     return pl.pallas_call(
         _kernel,
         out_shape=jax.ShapeDtypeStruct((T, D), BF),
-        in_specs=[vm, vm, hbm, hbm, hbm],
+        in_specs=[vm, vm, vm, hbm, hbm, hbm],
         out_specs=vm,
         scratch_shapes=[
-            pltpu.VMEM((N, 16, T), F32),
-            pltpu.VMEM((KC, N, T, KW), BF),
+            pltpu.VMEM((N, 8, T), jnp.int32),
+            pltpu.VMEM((N, 8, T), F32),
+            pltpu.VMEM((2, N, T, 256), BF),
+            pltpu.VMEM((3, N, T, 512), BF),
             pltpu.VMEM((N, RB, T), BF),
             pltpu.VMEM((N, 3 * T, RB), BF),
             pltpu.VMEM((EL + 1, N * CAP, KW), BF),
@@ -318,6 +348,7 @@
             pltpu.VMEM((NC, 2, 2, 64, NW), F32),
             pltpu.VMEM((NC, 2, 64, NW), F32),
             dma((N,)), dma((N,)),
+            dma((N,)), dma((N,)),
             dma((KC, N)), dma((KC, N)),
             dma((NS, 2)), dma((2,)),
             dma((NC,)), dma((NC,)),
@@ -326,13 +357,12 @@
         ],
         compiler_params=pltpu.CompilerParams(collective_id=0, has_side_effects=True, vmem_limit_bytes=67043328),
         name='moe',
-    )(tab, x, w1, w3, w2)
+    )(idx, g, x, w1, w3, w2)
 
 
 def solution(mesh):
     def local(x, idx, g, hot_tok, w1, w3, w2):
-        tab = jnp.concatenate([idx.T.astype(F32), g.T], axis=0)
-        return _moe(tab, x, w1, w3, w2)
+        return _moe(idx.T, g.T, x, w1, w3, w2)
 
     rows = P(('data', 'expert'))
     wspec = P('expert')

time: 89.6 us -> 86.5 us (0.965)
  other arithmetic: 1.97 us -> 0 us
  Pallas kernels: 85.5 us -> 84.5 us
    concatenate x1 -> x0, other arithmetic: 1.29 us -> none  [local(): tab = jnp.concatenate([idx.T.astype(F32), g.T], axis=0)]
    pallas_call x1, Pallas kernels: 85.5 us -> 84.5 us  [_moe(): pl.pallas_call(_kernel, out_shape=jax.ShapeDtypeStruct((T, D), BF), in_sp...]
where the time goes in v3:
time: 86.5 us; the launch traced here: 86.3 us
  Pallas kernels  84.5 us (98%)
  local copies, waits for them, and re-layouts  1.88 us (2%)
    pallas_call x1, Pallas kernels, _moe(): pl.pallas_call(_kernel, out_shape=jax.ShapeDtypeStruct((T, D), BF), in_sp...  84.5 us
    unnamed x1, local copies, waits for them, and re-layouts  1.88 us

profile of v3, /device:TPU:0, one launch (start us, length us, event | category | flops | bytes accessed | tf_op | source)
XLA Modules:
  0.0 86.3 jit_solution(14665310120761245234)
XLA Ops:
  0.0 84.5 %moe.1 = bf16[128,2048]{1,0:T(8,128)(2,1)} custom-call(s32[8,128]{1,0:T(8,128)} %bitcast.2, f32[8,128]{1,0:T(8,128)} %bitcast.3, bf16[128,2048]{1,0:T(8,128)(2,1)} %x_ref.1, bf16[8,2048,1024]{2,1,0:T(8,128)(2,1)} %w1_ref.1, bf16[8,2048,1024]{2,1,0:T(8,128)(2,1)} %w3_ref.1, bf16[8,1024,2048]{2,1,0:T(8,128)(2,1)} %w2_ref.1), custom_call_target="tpu_custom_call" | custom-call | tf_op jit(solution)/shard_map/moe/pallas_call | solution.py:329
  84.5 1.9 %copy.8 = bf16[128,2048]{1,0:T(8,128)(2,1)} copy(bf16[128,2048]{1,0:T(8,128)(2,1)} %moe.1) | data formatting | bytes 1048576

commit v4 on v3

--- a/solution.py
+++ b/solution.py
@@ -26,6 +26,7 @@
 NP = EL // EP
 NS = 3
 FWD_AT = 2
+AHEAD = 2
 CHIP = (0, 3, 1, 2)
 
 
@@ -33,9 +34,9 @@
     return jnp.dot(a, b, preferred_element_type=F32)
 
 
-def _kernel(idx_ref, g_ref, x_ref, w1_ref, w3_ref, w2_ref, y_ref,
-            idxs, gs, xsmall, xbig, onehot, gates, xs, acc, u, ring1, ring2, hbuf, r1, r2, r3,
-            tab_s, tab_r, gt_s, gt_r, ag_s, ag_r, w1_sem, w2_sem, d_s, d_r, s1_s, s1_r, s2_s, s2_r):
+def _kernel(idx_hbm, g_hbm, x_hbm, w1_ref, w3_ref, w2_ref, y_hbm,
+            idxs, gs, xsmall, xbig, onehot, gates, xs, acc, u, ring1, ring2, hbuf, r1, r2, r3, y_ref, y_sem,
+            tab_s, tab_r, gt_s, gt_r, ag_s, ag_r, w1_sem, w2_sem, own_sem, d_s, d_r, s1_s, s1_r, s2_s, s2_r):
     me = lax.axis_index('expert')
     core, xb, yb = me % 2, (me // 2) % 2, me // 4
 
@@ -56,42 +57,49 @@
     def down_copy(nc):
         return pltpu.make_async_copy(w2_ref.at[:, :, pl.ds(nc * NW, NW)], ring2.at[nc % 2], w2_sem.at[nc % 2])
 
+    barrier = pltpu.get_barrier_semaphore()
+    for mask in range(1, N):
+        pl.semaphore_signal(barrier, inc=1, device_id=peer(mask), device_id_type=pl.DeviceIdType.MESH)
+
+    def part(c, mask):
+        return xsmall.at[c, mask] if c < 2 else xbig.at[c - 2, mask]
+
+    own = [pltpu.make_async_copy(idx_hbm, idxs.at[0], own_sem.at[KC]),
+           pltpu.make_async_copy(g_hbm, gs.at[0], own_sem.at[KC + 1])]
+    for c in range(KC):
+        own.append(pltpu.make_async_copy(x_hbm.at[:, pl.ds(*CHUNKS[c])], part(c, 0), own_sem.at[c]))
+    for c in own:
+        c.start()
     for i in range(NS):
         for c in up_copies(0, i, i):
             c.start()
 
-    barrier = pltpu.get_barrier_semaphore()
-    for mask in range(1, N):
-        pl.semaphore_signal(barrier, inc=1, device_id=peer(mask), device_id_type=pl.DeviceIdType.MESH)
-    pl.semaphore_wait(barrier, N - 1)
-
     def table_copies(mask):
-        return (remote(idx_ref, idxs.at[mask], tab_s.at[mask], tab_r.at[mask], mask),
-                remote(g_ref, gs.at[mask], gt_s.at[mask], gt_r.at[mask], mask))
+        return (remote(idxs.at[0], idxs.at[mask], tab_s.at[mask], tab_r.at[mask], mask),
+                remote(gs.at[0], gs.at[mask], gt_s.at[mask], gt_r.at[mask], mask))
 
     def table_fwd(mask):
         return (remote(idxs.at[mask], idxs.at[mask + 1], tab_s.at[mask + 1], tab_r.at[mask + 1], 1),
                 remote(gs.at[mask], gs.at[mask + 1], gt_s.at[mask + 1], gt_r.at[mask + 1], 1))
 
-    def part(c, mask):
-        return xsmall.at[c, mask] if c < 2 else xbig.at[c - 2, mask]
-
     def ag_copy(c, mask):
-        return remote(x_ref.at[:, pl.ds(*CHUNKS[c])], part(c, mask), ag_s.at[c, mask], ag_r.at[c, mask], mask)
+        return remote(part(c, 0), part(c, mask), ag_s.at[c, mask], ag_r.at[c, mask], mask)
 
     def fwd_copy(c, mask):
         return remote(part(c, mask), part(c, mask + 1), ag_s.at[c, mask + 1], ag_r.at[c, mask + 1], 1)
 
+    for c in own:
+        c.wait()
+    pl.semaphore_wait(barrier, N - 1)
     for mask in (6, 2, 4, 1):
         for c in table_copies(mask):
             c.start()
-    for c in range(KC):
+    def send(c):
         for mask in (6, 2, 4, 1):
             ag_copy(c, mask).start()
-    idxs[0] = idx_ref[...]
-    gs[0] = g_ref[...]
-    for c, (first, width) in enumerate(CHUNKS):
-        part(c, 0)[...] = x_ref[:, first:first + width]
+
+    for c in range(AHEAD):
+        send(c)
     for mask in (2, 4, 6):
         for c in table_copies(mask):
             c.wait_recv()
@@ -120,48 +128,48 @@
     upper = jnp.where(upper, 1.0, 0.0).astype(BF)
     rank_all = jnp.where(sel_all > 0.5, _dot(sel_all.astype(BF), upper), -1.0)
 
-    col = lax.broadcasted_iota(jnp.int32, (32, RB), 1)
-    row = lax.broadcasted_iota(jnp.int32, (32, RB), 0)
-    owner = jnp.where(col < EL * CAP, col // CAP, 0)
-    pick = [jnp.where(row == q * EL + owner, 1.0, 0.0).astype(BF) for q in range(4)]
-    colt = lax.broadcasted_iota(jnp.int32, (T, RB), 1)
-    slot_of = jnp.where(colt < EL * CAP, colt % CAP, colt - EL * CAP + CAP).astype(F32)
     sub = lax.broadcasted_iota(jnp.int32, (CAP, T), 0).astype(F32)
     for r in range(N):
-        rk = rank_all[r * EL:(r + 1) * EL]
         for b in range(EL + 1):
             want = sub if b < EL else sub + CAP
-            src = b % EL
-            hit = jnp.broadcast_to(rk[src:src + 1], (CAP, T)) == want
+            at = r * EL + b % EL
+            hit = jnp.broadcast_to(rank_all[at:at + 1], (CAP, T)) == want
             onehot[r, b * CAP:(b + 1) * CAP, :] = jnp.where(hit, 1.0, 0.0).astype(BF)
-        g = weights[r]
-        g1 = jnp.minimum(g, BF_MAX).astype(BF).astype(F32)
-        rem = g - g1
-        g2 = rem.astype(BF).astype(F32)
-        g3 = rem - g2
-        v = jnp.concatenate([rk, g1, g2, g3], axis=0)
-        vt = v.T.astype(BF)
-        hit = _dot(vt, pick[0]) == slot_of
-        for q in range(3):
-            gates[r, q * T:(q + 1) * T, :] = jnp.where(hit, _dot(vt, pick[q + 1]), 0.0).astype(BF)
+
+    def build_gates():
+        col = lax.broadcasted_iota(jnp.int32, (32, RB), 1)
+        row = lax.broadcasted_iota(jnp.int32, (32, RB), 0)
+        owner = jnp.where(col < EL * CAP, col // CAP, 0)
+        pick = [jnp.where(row == q * EL + owner, 1.0, 0.0).astype(BF) for q in range(4)]
+        colt = lax.broadcasted_iota(jnp.int32, (T, RB), 1)
+        slot_of = jnp.where(colt < EL * CAP, colt % CAP, colt - EL * CAP + CAP).astype(F32)
+        for r in range(N):
+            g = weights[r]
+            g1 = jnp.minimum(g, BF_MAX).astype(BF).astype(F32)
+            rem = g - g1
+            g2 = rem.astype(BF).astype(F32)
+            g3 = rem - g2
+            v = jnp.concatenate([rank_all[r * EL:(r + 1) * EL], g1, g2, g3], axis=0)
+            vt = v.T.astype(BF)
+            hit = _dot(vt, pick[0]) == slot_of
+            for q in range(3):
+                gates[r, q * T:(q + 1) * T, :] = jnp.where(hit, _dot(vt, pick[q + 1]), 0.0).astype(BF)
 
     def forward(c):
         for mask in (2, 4, 6):
             ag_copy(c, mask).wait_recv()
             fwd_copy(c, mask).start()
+        if c + AHEAD < KC:
+            send(c + AHEAD)
 
     forward(0)
+    build_gates()
     for kc in range(KC):
         ag_copy(kc, 1).wait_recv()
         for mask in (2, 4, 6):
             fwd_copy(kc, mask).wait_recv()
 
         width = CHUNKS[kc][1]
-        for r in range(N):
-            rows = _dot(onehot[r], part(kc, r)[...]).astype(BF)
-            for b in range(EL + 1):
-                xs[b, r * CAP:(r + 1) * CAP, 0:width] = rows[b * CAP:(b + 1) * CAP]
-
         def block(b, slot, q, kc=kc, width=width):
             rows = xs[b, :, 0:width]
             for n in range(FF // 256):
@@ -177,17 +185,23 @@
                 else:
                     u[b, :, cols] = (jax.nn.silu(a) * bb).astype(BF)
 
-        def step(p, _, kc=kc):
+        def step(p, _, kc=kc, first=False):
             i = kc * NP + p
             slot = i % NS
             for c in up_copies(kc, p, slot):
                 c.wait()
+            if first:
+                for r in range(N):
+                    rows = _dot(onehot[r], part(kc, r)[...]).astype(BF)
+                    for b in range(EL + 1):
+                        xs[b, r * CAP:(r + 1) * CAP, 0:width] = rows[b * CAP:(b + 1) * CAP]
             for q in range(EP):
                 block(p * EP + q, slot, q)
 
-            @pl.when((p == 0) & (me == 0))
-            def _():
-                block(EL, slot, 0)
+            if first:
+                @pl.when(me == 0)
+                def _():
+                    block(EL, slot, 0)
 
             @pl.when(p < NP - NS)
             def _():
@@ -209,7 +223,8 @@
                 def _():
                     down_copy(p).start()
             return 0
-        lax.fori_loop(0, NP, step, 0)
+        step(jnp.int32(0), 0, first=True)
+        lax.fori_loop(1, NP, step, 0)
 
     def d_copy(nc):
         return remote(acc.at[nc % 2, pl.ds(4, 4), pl.ds(0, T), pl.ds(0, NW)], r1.at[nc], d_s.at[nc], d_r.at[nc], 1)
@@ -239,15 +254,19 @@
         r2[nc, 1, 1] = r2[nc, 1, 1] + r1[nc, 3, 64:128]
         sb.start()
 
+    def y_copy(nc):
+        at = pl.ds(pl.multiple_of(nc * NW, NW), NW)
+        return pltpu.make_async_copy(y_ref.at[nc], y_hbm.at[:, at], y_sem.at[nc])
+
     def final(nc):
         for h, c in enumerate(s2_copies(nc)):
             c.wait_recv()
             rows = slice(h * 64, h * 64 + 64)
             val = r1[nc, 0, rows] + r2[nc, h, 1 - h] + r3[nc, h]
-            y_ref[rows, pl.ds(pl.multiple_of(nc * NW, NW), NW)] = val.astype(BF)
+            y_ref[nc, rows] = val.astype(BF)
+        y_copy(nc).start()
 
     def out_step(nc, _):
-        down_copy(nc).wait()
 
         def put(b, e):
             h = _dot(u[b], ring2[nc % 2, e]).astype(BF)
@@ -264,6 +283,10 @@
         def _():
             down_copy(nc + 2).start()
 
+        @pl.when(nc + 1 < NC)
+        def _():
+            down_copy(nc + 1).wait()
+
         @pl.when(nc >= 1)
         def _():
             stage1(nc - 1)
@@ -295,6 +318,7 @@
         def _():
             final(nc - 5)
         return 0
+    down_copy(0).wait()
     lax.fori_loop(0, NC, out_step, 0)
     stage1(NC - 1)
     stage2(NC - 3)
@@ -321,16 +345,17 @@
             d_copy(nc).wait_send()
         for c in s1_copies(nc) + s2_copies(nc):
             c.wait_send()
+        y_copy(nc).wait()
 
 
 def _moe(idx, g, x, w1, w3, w2):
     dma = pltpu.SemaphoreType.DMA
-    vm, hbm = pl.BlockSpec(memory_space=pltpu.VMEM), pl.BlockSpec(memory_space=pl.ANY)
+    hbm = pl.BlockSpec(memory_space=pl.ANY)
     return pl.pallas_call(
         _kernel,
         out_shape=jax.ShapeDtypeStruct((T, D), BF),
-        in_specs=[vm, vm, vm, hbm, hbm, hbm],
-        out_specs=vm,
+        in_specs=[hbm] * 6,
+        out_specs=hbm,
         scratch_shapes=[
             pltpu.VMEM((N, 8, T), jnp.int32),
             pltpu.VMEM((N, 8, T), F32),
@@ -347,10 +372,12 @@
             pltpu.VMEM((NC, 4, T, NW), F32),
             pltpu.VMEM((NC, 2, 2, 64, NW), F32),
             pltpu.VMEM((NC, 2, 64, NW), F32),
+            pltpu.VMEM((NC, T, NW), BF),
+            dma((NC,)),
             dma((N,)), dma((N,)),
             dma((N,)), dma((N,)),
             dma((KC, N)), dma((KC, N)),
-            dma((NS, 2)), dma((2,)),
+            dma((NS, 2)), dma((2,)), dma((KC + 2,)),
             dma((NC,)), dma((NC,)),
             dma((NC, 2)), dma((NC, 2)),
             dma((NC, 2)), dma((NC, 2)),

time: 86.5 us -> 84.8 us (0.980)
  Pallas kernels: 84.5 us -> 82.7 us
    pallas_call x1, Pallas kernels: 84.5 us -> 82.7 us  [_moe(): pl.pallas_call(_kernel, out_shape=jax.ShapeDtypeStruct((T, D), BF), in_sp...]
where the time goes in v4:
time: 84.8 us; the launch traced here: 84.6 us
  Pallas kernels  82.7 us (98%)
  local copies, waits for them, and re-layouts  1.88 us (2%)
    pallas_call x1, Pallas kernels, _moe(): pl.pallas_call(_kernel, out_shape=jax.ShapeDtypeStruct((T, D), BF), in_sp...  82.7 us
    unnamed x1, local copies, waits for them, and re-layouts  1.88 us

profile of v4, /device:TPU:0, one launch (start us, length us, event | category | flops | bytes accessed | tf_op | source)
XLA Modules:
  0.0 84.6 jit_solution(6553883571303639016)
XLA Ops:
  0.0 82.7 %moe.1 = bf16[128,2048]{1,0:T(8,128)(2,1)} custom-call(s32[8,128]{1,0:T(8,128)} %bitcast.2, f32[8,128]{1,0:T(8,128)} %bitcast.3, bf16[128,2048]{1,0:T(8,128)(2,1)} %x_hbm.1, bf16[8,2048,1024]{2,1,0:T(8,128)(2,1)} %w1_ref.1, bf16[8,2048,1024]{2,1,0:T(8,128)(2,1)} %w3_ref.1, bf16[8,1024,2048]{2,1,0:T(8,128)(2,1)} %w2_ref.1), custom_call_target="tpu_custom_call" | custom-call | tf_op jit(solution)/shard_map/moe/pallas_call | solution.py:354
  82.7 1.9 %copy.8 = bf16[128,2048]{1,0:T(8,128)(2,1)} copy(bf16[128,2048]{1,0:T(8,128)(2,1)} %moe.1) | data formatting | bytes 1048576

commit v5 on v4

--- a/solution.py
+++ b/solution.py
@@ -35,8 +35,8 @@
 
 
 def _kernel(idx_hbm, g_hbm, x_hbm, w1_ref, w3_ref, w2_ref, y_hbm,
-            idxs, gs, xsmall, xbig, onehot, gates, xs, acc, u, ring1, ring2, hbuf, r1, r2, r3, y_ref, y_sem,
-            tab_s, tab_r, gt_s, gt_r, ag_s, ag_r, w1_sem, w2_sem, own_sem, d_s, d_r, s1_s, s1_r, s2_s, s2_r):
+            idxs, gs, xsmall, xbig, onehot, gates, xs, acc, u, ring1, ring2, r1, r2, r3, y_ref, y_sem,
+            tab_s, tab_r, gt_s, gt_r, ag_s, ag_r, w1_sem, w2_sem, own_sem, d_s, d_r, s1_s, s1_r, s2_s, s2_r, l1_s, l1_r, l2_s, l2_r):
     me = lax.axis_index('expert')
     core, xb, yb = me % 2, (me // 2) % 2, me // 4
 
@@ -58,7 +58,7 @@
         return pltpu.make_async_copy(w2_ref.at[:, :, pl.ds(nc * NW, NW)], ring2.at[nc % 2], w2_sem.at[nc % 2])
 
     barrier = pltpu.get_barrier_semaphore()
-    for mask in range(1, N):
+    for mask in (1, 2, 4, 6):
         pl.semaphore_signal(barrier, inc=1, device_id=peer(mask), device_id_type=pl.DeviceIdType.MESH)
 
     def part(c, mask):
@@ -70,9 +70,6 @@
         own.append(pltpu.make_async_copy(x_hbm.at[:, pl.ds(*CHUNKS[c])], part(c, 0), own_sem.at[c]))
     for c in own:
         c.start()
-    for i in range(NS):
-        for c in up_copies(0, i, i):
-            c.start()
 
     def table_copies(mask):
         return (remote(idxs.at[0], idxs.at[mask], tab_s.at[mask], tab_r.at[mask], mask),
@@ -90,7 +87,7 @@
 
     for c in own:
         c.wait()
-    pl.semaphore_wait(barrier, N - 1)
+    pl.semaphore_wait(barrier, 4)
     for mask in (6, 2, 4, 1):
         for c in table_copies(mask):
             c.start()
@@ -100,6 +97,9 @@
 
     for c in range(AHEAD):
         send(c)
+    for i in range(NS):
+        for c in up_copies(0, i, i):
+            c.start()
     for mask in (2, 4, 6):
         for c in table_copies(mask):
             c.wait_recv()
@@ -237,6 +237,46 @@
         return (remote(r2.at[nc, 0, 0], r3.at[nc, 0], s2_s.at[nc, 0], s2_r.at[nc, 0], 4),
                 remote(r2.at[nc, 1, 1], r3.at[nc, 1], s2_s.at[nc, 1], s2_r.at[nc, 1], 2))
 
+    LAST = NC - 1
+
+    def last1_copies(h):
+        cols = pl.ds(h * 128, 128)
+        return (remote(r1.at[LAST, pl.ds(2, 2), pl.ds(0, 64), cols], r2.at[LAST, 0, :, :, cols], l1_s.at[h, 0], l1_r.at[h, 0], 2),
+                remote(r1.at[LAST, pl.ds(1, 2), pl.ds(64, 64), cols], r2.at[LAST, 1, :, :, cols], l1_s.at[h, 1], l1_r.at[h, 1], 4))
+
+    def last2_copies(h):
+        cols = pl.ds(h * 128, 128)
+        return (remote(r2.at[LAST, 0, 0, :, cols], r3.at[LAST, 0, :, cols], l2_s.at[h, 0], l2_r.at[h, 0], 4),
+                remote(r2.at[LAST, 1, 1, :, cols], r3.at[LAST, 1, :, cols], l2_s.at[h, 1], l2_r.at[h, 1], 2))
+
+    def last1(h):
+        cols = slice(h * 128, h * 128 + 128)
+        for q in (2, 3, 1, 0):
+            r1[LAST, q, :, cols] = r1[LAST, q, :, cols] + acc[LAST % 2, q, 0:T, cols]
+        for c in last1_copies(h):
+            c.start()
+
+    def last2(h):
+        cols = slice(h * 128, h * 128 + 128)
+        ca, cb = last1_copies(h)
+        sa, sb = last2_copies(h)
+        ca.wait_recv()
+        r2[LAST, 0, 0, :, cols] = r2[LAST, 0, 0, :, cols] + r1[LAST, 1, 0:64, cols]
+        sa.start()
+        cb.wait_recv()
+        r2[LAST, 1, 1, :, cols] = r2[LAST, 1, 1, :, cols] + r1[LAST, 3, 64:128, cols]
+        sb.start()
+
+    def last_final():
+        for h in range(2):
+            cols = slice(h * 128, h * 128 + 128)
+            for k, c in enumerate(last2_copies(h)):
+                c.wait_recv()
+                rows = slice(k * 64, k * 64 + 64)
+                val = r1[LAST, 0, rows, cols] + r2[LAST, k, 1 - k, :, cols] + r3[LAST, k, :, cols]
+                y_ref[LAST, rows, cols] = val.astype(BF)
+        y_copy(LAST).start()
+
     def stage1(nc):
         d_copy(nc).wait_recv()
         for q in range(4):
@@ -271,7 +311,10 @@
         def put(b, e):
             h = _dot(u[b], ring2[nc % 2, e]).astype(BF)
             for r in range(N):
-                hbuf[r, b * CAP:(b + 1) * CAP, :] = h[r * CAP:(r + 1) * CAP]
+                if b < EL:
+                    xs[r, b * CAP:(b + 1) * CAP, 0:NW] = h[r * CAP:(r + 1) * CAP]
+                else:
+                    xs[r, 0:CAP, NW:2 * NW] = h[r * CAP:(r + 1) * CAP]
         for e in range(EL):
             put(e, e)
 
@@ -295,20 +338,22 @@
         def _():
             d_copy(nc - 2).wait_send()
 
-        def combine(rows):
+        def combine(second):
             for r in (1, 3, 5, 7, 0, 2, 4, 6):
-                z = _dot(gates[r, :, 0:rows], hbuf[r, 0:rows, :])
+                z = _dot(gates[r, :, 0:EL * CAP], xs[r, :, 0:NW])
+                if second:
+                    z = z + _dot(gates[r, :, EL * CAP:RB], xs[r, 0:CAP, NW:2 * NW])
                 acc[nc % 2, 4 * (r % 2) + CHIP[r // 2], 0:T, 0:NW] = z[0:T] + z[T:2 * T] + z[2 * T:3 * T]
                 if r == 7:
                     d_copy(nc).start()
 
         @pl.when(me == 0)
         def _():
-            combine(RB)
+            combine(True)
 
         @pl.when(me != 0)
         def _():
-            combine(EL * CAP)
+            combine(False)
 
         @pl.when(nc >= 3)
         def _():
@@ -320,14 +365,18 @@
         return 0
     down_copy(0).wait()
     lax.fori_loop(0, NC, out_step, 0)
-    stage1(NC - 1)
+    d_copy(LAST).wait_recv()
+    last1(0)
+    last1(1)
     stage2(NC - 3)
     final(NC - 5)
     stage2(NC - 2)
     final(NC - 4)
-    stage2(NC - 1)
-    for nc in range(NC - 3, NC):
-        final(nc)
+    last2(0)
+    last2(1)
+    final(NC - 3)
+    final(NC - 2)
+    last_final()
 
     for mask in (1, 2, 4, 6):
         for c in table_copies(mask):
@@ -343,9 +392,13 @@
     for nc in range(NC):
         if nc >= NC - 2:
             d_copy(nc).wait_send()
-        for c in s1_copies(nc) + s2_copies(nc):
+        if nc < LAST:
+            for c in s1_copies(nc) + s2_copies(nc):
+                c.wait_send()
+        y_copy(nc).wait()
+    for h in range(2):
+        for c in last1_copies(h) + last2_copies(h):
             c.wait_send()
-        y_copy(nc).wait()
 
 
 def _moe(idx, g, x, w1, w3, w2):
@@ -368,7 +421,6 @@
             pltpu.VMEM((EL + 1, N * CAP, FF), BF),
             pltpu.VMEM((NS, 2, EP, KW, FF), BF),
             pltpu.VMEM((2, EL, FF, NW), BF),
-            pltpu.VMEM((N, RB, NW), BF),
             pltpu.VMEM((NC, 4, T, NW), F32),
             pltpu.VMEM((NC, 2, 2, 64, NW), F32),
             pltpu.VMEM((NC, 2, 64, NW), F32),
@@ -381,6 +433,8 @@
             dma((NC,)), dma((NC,)),
             dma((NC, 2)), dma((NC, 2)),
             dma((NC, 2)), dma((NC, 2)),
+            dma((2, 2)), dma((2, 2)),
+            dma((2, 2)), dma((2, 2)),
         ],
         compiler_params=pltpu.CompilerParams(collective_id=0, has_side_effects=True, vmem_limit_bytes=67043328),
         name='moe',

time: 84.8 us -> 83.4 us (0.983)
  Pallas kernels: 82.7 us -> 81.2 us
    pallas_call x1, Pallas kernels: 82.7 us -> 81.2 us  [_moe(): pl.pallas_call(_kernel, out_shape=jax.ShapeDtypeStruct((T, D), BF), in_sp...]
where the time goes in v5:
time: 83.4 us; the launch traced here: 83.1 us
  Pallas kernels  81.2 us (97%)
  local copies, waits for them, and re-layouts  1.88 us (2%)
    pallas_call x1, Pallas kernels, _moe(): pl.pallas_call(_kernel, out_shape=jax.ShapeDtypeStruct((T, D), BF), in_sp...  81.2 us
    unnamed x1, local copies, waits for them, and re-layouts  1.88 us

profile of v5, /device:TPU:0, one launch (start us, length us, event | category | flops | bytes accessed | tf_op | source)
XLA Modules:
  0.0 83.1 jit_solution(193207982088358791)
XLA Ops:
  0.0 81.2 %moe.1 = bf16[128,2048]{1,0:T(8,128)(2,1)} custom-call(s32[8,128]{1,0:T(8,128)} %bitcast.2, f32[8,128]{1,0:T(8,128)} %bitcast.3, bf16[128,2048]{1,0:T(8,128)(2,1)} %x_hbm.1, bf16[8,2048,1024]{2,1,0:T(8,128)(2,1)} %w1_ref.1, bf16[8,2048,1024]{2,1,0:T(8,128)(2,1)} %w3_ref.1, bf16[8,1024,2048]{2,1,0:T(8,128)(2,1)} %w2_ref.1), custom_call_target="tpu_custom_call" | custom-call | tf_op jit(solution)/shard_map/moe/pallas_call | solution.py:407
  81.2 1.9 %copy.8 = bf16[128,2048]{1,0:T(8,128)(2,1)} copy(bf16[128,2048]{1,0:T(8,128)(2,1)} %moe.1) | data formatting | bytes 1048576
